TPU v7x, 32 devices: a whole 2x2x4 slice. The times are simulated.
32 devices in a mesh: gx: 4 (over z), gy: 8 (over y, x, core).
Axes of the slice: x: 2, y: 2, z: 4, core: 2. Of those that a mesh axis runs over, the one named last changes fastest.
Arguments:
- rhs: float32 [4, 8, 1, 3, 200, 128], P('gx', 'gy'), may hold values from -25 to 25
- stiff_inverse: bfloat16 [4, 8, 1, 1200, 1200], P('gx', 'gy'), may hold values from -2 to 6, as said below
- schur: bfloat16 [4, 8, 1, 1200, 1200], P('gx', 'gy'), may hold values from -2 to 6, as said below
- phi: bfloat16 [4, 8, 1, 24, 1200], P('gx', 'gy'), may hold values from -0.1875 to 0.1875
- coarse_inverse: float32 [192, 192], P(('gx', 'gy')), may hold values from -2 to 6, as said below
- incidence: int32 [4, 8, 1, 8], P('gx', 'gy'), may hold values from 0 to 63, as said below
- pairing: int32 [4, 8, 1, 3, 200], P('gx', 'gy'), may hold values from 0 to 199, as said below
Outputs:
- multipliers: float32 [4, 8, 1, 3, 200, 128], P('gx', 'gy')
- reduction: float32 [128], replicated
Inputs may be any that keep to these rules, and one draw needn't show every extreme that they name: `stiff_inverse`: each block is symmetric positive definite. `schur`: each block is symmetric positive definite. `coarse_inverse`: symmetric positive definite. `incidence`: the corners of the subdomain grid, periodic in the first two dimensions, under an arbitrary numbering of the 64 nodes: corner c of subdomain (x, y, z) is the grid point (x + c % 2, y + (c // 2) % 2, z + c // 4), and subdomains that share a grid point name the same node. `pairing`: each row over the last dimension is a permutation of 0 to 199.
All inputs are finite; a program needn't handle non-finite values.
Results may differ from a plain program's by a relative error of at most 0.0027.
Values sent between devices are 32-bit elements; how exact they have to be, the bound alone decides.
A program may use at most 64 MiB of HBM per device.

v0:
```python
import jax
import jax.numpy as jnp
from jax import lax
from jax.sharding import PartitionSpec as P

ITERS = 2


largest_index = lax.Precision.HIGHEST


def passed_along(array, axis, by):
    peers = lax.axis_size(axis)
    return lax.ppermute(array, axis, [(i, (i + by) % peers) for i in range(peers)])


def local(rhs, stiff_inverse, schur, phi, coarse_inverse, incidence, pairing):
    blocks = rhs.shape[2]
    face_dofs = rhs.shape[4]
    load_cases = rhs.shape[5]
    interface = 6 * face_dofs
    stiffness = stiff_inverse[0, 0]
    schur_block_stack = schur[0, 0]
    coupling_matrix = phi[0, 0].astype(jnp.float32)
    local_ids = incidence[0, 0]
    level = jnp.arange(blocks)[:, None]
    axis_id = jnp.arange(3)[None, :]
    active = jnp.where((level == blocks - 1) & (axis_id == 2), 0.0, 1.0).astype(jnp.float32)[
        :, :, None, None
    ]
    perm_table = (pairing[0, 0][..., None] == jnp.arange(face_dofs)[None, None, None, :]).astype(
        jnp.float32
    )
    owner_weights = None
    own_ids = jnp.concatenate([local_ids[:, 0], local_ids[-1:, 4]])
    own_dofs = (3 * own_ids[:, None] + jnp.arange(3, dtype=jnp.int32)[None, :]).reshape(-1)
    picked = jnp.take(
        lax.all_gather(coarse_inverse, ("gx", "gy"), axis=0, tiled=True), own_dofs, axis=1
    )
    every_owner = lax.all_gather(own_ids, ("gx", "gy"), axis=0, tiled=True)
    gathered_dofs = (3 * every_owner[:, None] + jnp.arange(3, dtype=jnp.int32)[None, :]).reshape(-1)
    owner_weights = jnp.take(picked, gathered_dofs, axis=0)

    def transpose_jump(values):
        masked = values * active
        moved = jnp.einsum("sakj,sakr->sajr", perm_table, masked, precision=largest_index)
        lower_x = passed_along(moved[:, 0], "gx", 1)
        lower_y = passed_along(moved[:, 1], "gy", 1)
        lower_z = jnp.concatenate([jnp.zeros_like(moved[:1, 2]), moved[:-1, 2]], axis=0)
        return jnp.stack(
            [-lower_x, masked[:, 0], -lower_y, masked[:, 1], -lower_z, masked[:, 2]], axis=1
        )

    def jump_field(field):
        upper_x = passed_along(field[:, 0], "gx", -1)
        upper_y = passed_along(field[:, 2], "gy", -1)
        upper_z = jnp.concatenate([field[1:, 4], jnp.zeros_like(field[:1, 4])], axis=0)
        neighbour = jnp.stack([upper_x, upper_y, upper_z], axis=1)
        paired = jnp.einsum("sakj,sajr->sakr", perm_table, neighbour, precision=largest_index)
        higher = jnp.stack([field[:, 1], field[:, 3], field[:, 5]], axis=1)
        return (higher - paired) * active

    def apply_local(matrices, field):
        low_field = field.reshape(blocks, interface, load_cases).astype(jnp.bfloat16)
        result = jnp.einsum("snm,smr->snr", matrices, low_field, preferred_element_type=jnp.float32)
        return result.reshape(blocks, 6, face_dofs, load_cases)

    def precondition(values):
        field = 0.5 * transpose_jump(values)
        return 0.5 * jump_field(apply_local(schur_block_stack, field))

    def inner_product(left, right):
        return jnp.sum(left * right, axis=(0, 1, 2))

    def energy_total(partial_value):
        return lax.psum(partial_value, ("gx", "gy"))

    residual = rhs[0, 0] * active
    multipliers = jnp.zeros_like(residual)
    preconditioned = precondition(residual)
    partial_energy = inner_product(residual, preconditioned)
    energy = energy_total(partial_energy)
    direction_field = None
    search_corner_values = None
    start_energy = energy
    direction = preconditioned
    for iteration in range(ITERS):
        direction_field = transpose_jump(direction)
        split = jnp.einsum(
            "vzh,vhq->vzq",
            coupling_matrix,
            direction_field.reshape(blocks, interface, load_cases),
            precision=largest_index,
        ).reshape(blocks, 2, 2, 2, 3, load_cases)
        empty = jnp.zeros((1, 2, 2, 3, load_cases), jnp.float32)
        by_node = jnp.concatenate([split[:, 0], empty], axis=0) + jnp.concatenate(
            [empty, split[:, 1]], axis=0
        )
        from_x = passed_along(by_node[:, :, 1], "gx", 1)
        along_x = by_node[:, :, 0] + from_x
        from_y = passed_along(along_x[:, 1], "gy", 1)
        owned = (along_x[:, 0] + from_y).reshape(-1, load_cases)
        gathered = lax.all_gather(owned, ("gx", "gy"), axis=0, tiled=True)
        solved = jnp.dot(owner_weights.T, gathered, precision=largest_index).reshape(
            blocks + 1, 3, load_cases
        )
        from_upper_x = passed_along(solved, "gx", -1)
        pair = jnp.stack([solved, from_upper_x], axis=0)
        from_upper_y = passed_along(pair, "gy", -1)
        quad = jnp.stack([pair, from_upper_y], axis=0)
        neighbour_values = jnp.stack([quad[:, :, :blocks], quad[:, :, 1:]], axis=0)
        neighbour_values = jnp.transpose(neighbour_values, (3, 0, 1, 2, 4, 5)).reshape(
            blocks, -1, load_cases
        )
        search_corner_values = neighbour_values
        spread_operator = jnp.einsum(
            "xgy,xgh->xyh", coupling_matrix, search_corner_values, precision=largest_index
        )
        displacement = apply_local(stiffness, direction_field) + spread_operator.reshape(
            blocks, 6, face_dofs, load_cases
        )
        product_field = jump_field(displacement)
        curvature = lax.psum(inner_product(direction, product_field), ("gx", "gy"))
        alpha = energy / curvature
        multipliers = multipliers + alpha * direction
        residual = residual - alpha * product_field
        preconditioned = precondition(residual)
        partial_energy = inner_product(residual, preconditioned)
        if iteration + 1 < ITERS:
            energy_next = energy_total(partial_energy)
            ratio = energy_next / energy
            direction = preconditioned + ratio * direction
        else:
            energy_next = energy_total(partial_energy)
        energy = energy_next
    return (multipliers[None, None], energy / start_energy)


def solution(mesh):
    return jax.shard_map(
        local,
        mesh=mesh,
        in_specs=(
            P("gx", "gy", None, None, None, None),
            P("gx", "gy", None, None, None),
            P("gx", "gy", None, None, None),
            P("gx", "gy", None, None, None),
            P(("gx", "gy"), None),
            P("gx", "gy", None, None),
            P("gx", "gy", None, None, None),
        ),
        out_specs=(P("gx", "gy", None, None, None, None), P()),
        check_vma=False,
    )
```

profile of v0, /device:TPU:0, one launch (start us, length us, event | category | flops | bytes accessed | tf_op | source)
XLA Modules:
  0.0 463.3 jit_solution(669811901619081959)
XLA Ops:
  1.5 1.9 convolution_bitcast_fusion.4
  4.6 2.6 collective-permute-start
  7.1 1.4 fusion.99
  8.5 1.3 broadcast_multiply_fusion.1
  10.1 1.8 fusion.32
  11.9 1.4 fusion.96
  13.3 40.4 %all-reduce.4 = s32[64]{0:T(128)S(1)} all-reduce(s32[64]{0:T(128)S(1)} %fusion.96), channel_id=1, replica_groups=mesh['gx'=4,'gy'=8] {'gx','gy'}, use_global_device_ids=true, to_apply=%add.4 | all-reduce | flops 64 | bytes 512
  53.9 41.3 %all-gather = f32[32,6,192]{2,1,0:T(8,128)S(1)} all-gather(f32[1,6,192]{2,1,0:T(8,128)} %bitcast.317), channel_id=1, replica_groups=mesh['gx'=4,'gy'=8] {'gx','gy'}, dimensions={0}, use_global_device_ids=true | all-gather | bytes 152064 | tf_op jit(solution)/shard_map/all_gather | solution.py:38
  95.9 1.0 copy.41
  99.0 0.9 bitcast_dynamic-update-slice_fusion.9
  99.9 0.9 slice_dynamic-update-slice_fusion.14
  100.8 0.9 bitcast_dynamic-update-slice_fusion.8
  101.7 0.9 slice_dynamic-update-slice_fusion.13
  102.6 0.9 slice_dynamic-update-slice_fusion.12
  103.6 2.8 fusion
  106.6 5.0 %collective-permute-done.2 = f32[1,200,128]{2,1,0:T(8,128)S(1)} collective-permute-done((f32[1,200,128]{2,1,0:T(8,128)S(1)}, f32[1,200,128]{2,1,0:T(8,128)S(1)}, u32[]{:S(2)}, u32[]{:S(2)}) %collective-permute-start.2) | collective-permute-done | bytes 102432 | tf_op jit(solution)/shard_map/ppermute | solution.py:14
  114.1 5.6 %collective-permute-done.4 = f32[1,200,128]{2,1,0:T(8,128)S(1)} collective-permute-done((f32[1,200,128]{2,1,0:T(8,128)S(1)}, f32[1,200,128]{2,1,0:T(8,128)S(1)}, u32[]{:S(2)}, u32[]{:S(2)}) %collective-permute-start.4) | collective-permute-done | bytes 102432 | tf_op jit(solution)/shard_map/ppermute | solution.py:14
  121.6 4.9 %collective-permute-done.6 = f32[2,2,3,128]{3,2,1,0:T(4,128)S(1)} collective-permute-done((f32[2,2,3,128]{3,2,1,0:T(4,128)S(1)}, f32[2,2,3,128]{3,2,1,0:T(4,128)S(1)}, u32[]{:S(2)}, u32[]{:S(2)}) %collective-permute-start.6) | collective-permute-done | bytes 6176 | tf_op jit(solution)/shard_map/ppermute | solution.py:14
  127.9 1.3 gather_fusion.1
  129.2 2.1 collective-permute-done.7
  132.0 39.4 %all-gather.1 = f32[32,6,128]{2,1,0:T(8,128)} all-gather(f32[1,6,128]{2,1,0:T(8,128)S(1)} %reshape.812), channel_id=1, replica_groups=mesh['gx'=4,'gy'=8] {'gx','gy'}, dimensions={0}, use_global_device_ids=true | all-gather | bytes 101376 | tf_op jit(solution)/shard_map/all_gather | solution.py:103
  171.3 0.9 reshape.813
  172.3 1.2 fusion.60
  173.6 3.6 collective-permute-done.8
  177.9 1.9 convert_element_type.109
  182.4 2.0 fusion.7
  184.4 3.2 collective-permute-start.10
  187.5 2.0 collective-permute-start.11
  190.2 1.6 collective-permute-done.11
  191.8 1.3 multiply_reduce_fusion.2
  193.0 38.4 %all-reduce.5 = (f32[128]{0:T(128)S(1)}, f32[128]{0:T(128)S(1)}) all-reduce(f32[128]{0:T(128)S(1)} %get-tuple-element.3, f32[128]{0:T(128)S(1)} %get-tuple-element.2), channel_id=1, replica_groups=mesh['gx'=4,'gy'=8] {'gx','gy'}, use_global_device_ids=true, to_apply=%region_1.2 | all-reduce | flops 256 | bytes 2048 | tf_op jit(solution)/shard_map/psum | solution.py:76
  232.0 1.5 multiply_bitcast_fusion.2
  234.4 2.2 collective-permute-start.12
  236.6 4.3 collective-permute-done.12
  241.7 1.0 fusion.2
  242.7 1.7 collective-permute-start.14
  244.5 3.0 collective-permute-done.14
  247.5 1.8 multiply_reduce_fusion.1
  249.3 39.4 %psum.37 = f32[128]{0:T(128)S(1)} all-reduce(f32[128]{0:T(128)} %get-tuple-element.65), channel_id=1, replica_groups=mesh['gx'=4,'gy'=8] {'gx','gy'}, use_global_device_ids=true, to_apply=%region_5.6 | all-reduce | flops 128 | bytes 1024 | tf_op jit(solution)/shard_map/psum | solution.py:76
  288.7 1.1 multiply_bitcast_fusion.1
  290.7 2.1 collective-permute-start.16
  292.7 4.5 collective-permute-done.16
  299.0 1.4 collective-permute-start.18
  300.4 4.1 collective-permute-done.18
  304.5 3.9 collective-permute-done.19
  308.4 40.7 %all-gather.2 = f32[32,6,128]{2,1,0:T(8,128)} all-gather(f32[1,6,128]{2,1,0:T(8,128)S(1)} %reshape.814), channel_id=1, replica_groups=mesh['gx'=4,'gy'=8] {'gx','gy'}, dimensions={0}, use_global_device_ids=true | all-gather | bytes 101376 | tf_op jit(solution)/shard_map/all_gather | solution.py:103
  349.1 1.5 reshape.815
  350.7 1.2 fusion.58
  352.0 3.6 collective-permute-done.20
  355.6 1.8 convert_element_type.113
  357.5 1.4 fusion.64
  358.9 1.9 fusion.6
  360.9 1.9 collective-permute-start.22
  362.8 1.8 collective-permute-start.23
  364.6 1.6 collective-permute-done.22
  366.9 1.2 multiply_reduce_fusion
  368.1 38.5 %psum.38 = f32[128]{0:T(128)S(1)} all-reduce(f32[128]{0:T(128)S(1)} %get-tuple-element.67), channel_id=1, replica_groups=mesh['gx'=4,'gy'=8] {'gx','gy'}, use_global_device_ids=true, to_apply=%region_7.8 | all-reduce | flops 128 | bytes 1024 | tf_op jit(solution)/shard_map/psum | solution.py:123
  406.6 2.1 multiply_bitcast_fusion
  409.6 2.2 collective-permute-start.24
  411.8 4.3 collective-permute-done.24
  416.9 1.0 fusion.4
  417.9 1.8 collective-permute-start.26
  419.7 3.0 collective-permute-done.26
  423.2 39.6 %psum.39 = f32[128]{0:T(128)S(1)} all-reduce(f32[128]{0:T(128)S(1)} %fusion.16), channel_id=1, replica_groups=mesh['gx'=4,'gy'=8] {'gx','gy'}, use_global_device_ids=true, to_apply=%region_9.10 | all-reduce | flops 128 | bytes 1024 | tf_op jit(solution)/shard_map/psum | solution.py:76
  (183 shorter events, 24.4 us)
Async XLA Ops:
  0.6 181.7 %copy-start = (bf16[1,1,1,1200,1200]{4,3,2,1,0:T(8,128)(2,1)S(1)}, bf16[1,1,1,1200,1200]{4,3,2,1,0:T(8,128)(2,1)}, u32[]{:S(2)}) copy-start(bf16[1,1,1,1200,1200]{4,3,2,1,0:T(8,128)(2,1)} %param.8) | copy-start | bytes 8640004
  0.7 111.0 %copy-start.12 = (f32[3]{0:T(128)}, f32[3]{0:T(128)S(1)}, u32[]{:S(2)}) copy-start(f32[3]{0:T(128)S(1)} %compare_select_fusion.4) | copy-start | bytes 40
  4.1 96.7 %collective-permute-start.1 = (f32[1,200,128]{2,1,0:T(8,128)S(1)}, f32[1,200,128]{2,1,0:T(8,128)}, u32[]{:S(2)}, u32[]{:S(2)}) collective-permute-start(f32[1,200,128]{2,1,0:T(8,128)S(1)} %get-tuple-element.47), channel_id=1, source_target_pairs={{0,1},{1,2},{2,3},{3,4},{4,5},{5,6},{6,7},{7,0},{8,9},{9,10},{10,1... | collective-permute-start | bytes 307208 | tf_op jit(solution)/shard_map/ppermute | solution.py:14
  4.6 94.4 %collective-permute-start = (f32[1,200,128]{2,1,0:T(8,128)}, f32[1,200,128]{2,1,0:T(8,128)}, u32[]{:S(2)}, u32[]{:S(2)}) collective-permute-start(f32[1,200,128]{2,1,0:T(8,128)} %get-tuple-element.48), channel_id=1, source_target_pairs={{0,8},{8,16},{16,24},{24,0},{1,9},{9,17},{17,25},{25,1},{2,10},{10... | collective-permute-start | bytes 307208 | tf_op jit(solution)/shard_map/ppermute | solution.py:14
  99.0 12.7 %copy-start.20 = (f32[3]{0:T(128)}, f32[3]{0:T(128)S(1)}, u32[]{:S(2)}) copy-start(f32[3]{0:T(128)S(1)} %pad.44.clone) | copy-start | bytes 40
  106.4 14.1 %copy-start.11 = (bf16[1,1,1,24,1200]{4,3,2,1,0:T(8,128)(2,1)S(1)}, bf16[1,1,1,24,1200]{4,3,2,1,0:T(8,128)(2,1)}, u32[]{:S(2)}) copy-start(bf16[1,1,1,24,1200]{4,3,2,1,0:T(8,128)(2,1)} %param.10) | copy-start | bytes 172804
  106.4 20.6 %copy-start.16 = (s32[192,1]{0,1:T(1,128)S(1)}, s32[192,1]{0,1:T(1,128)}, u32[]{:S(2)}) copy-start(s32[192,1]{0,1:T(1,128)} %compare_select_fusion) | copy-start | bytes 2308
  106.5 5.2 %collective-permute-start.2 = (f32[1,200,128]{2,1,0:T(8,128)S(1)}, f32[1,200,128]{2,1,0:T(8,128)S(1)}, u32[]{:S(2)}, u32[]{:S(2)}) collective-permute-start(f32[1,200,128]{2,1,0:T(8,128)S(1)} %get-tuple-element.34), channel_id=1, source_target_pairs={{0,24},{8,0},{16,8},{24,16},{1,25},{9,1},{17,9},{25,17},{2,26},{10... | collective-permute-start | bytes 307208 | tf_op jit(solution)/shard_map/ppermute | solution.py:14
  106.6 5.1 %collective-permute-start.3 = (f32[1,200,128]{2,1,0:T(8,128)S(1)}, f32[1,200,128]{2,1,0:T(8,128)S(1)}, u32[]{:S(2)}, u32[]{:S(2)}) collective-permute-start(f32[1,200,128]{2,1,0:T(8,128)S(1)} %get-tuple-element.35), channel_id=1, source_target_pairs={{0,7},{1,0},{2,1},{3,2},{4,3},{5,4},{6,5},{7,6},{8,15},{9,8},{10,9... | collective-permute-start | bytes 307208 | tf_op jit(solution)/shard_map/ppermute | solution.py:14
  113.1 6.5 %collective-permute-start.4 = (f32[1,200,128]{2,1,0:T(8,128)S(1)}, f32[1,200,128]{2,1,0:T(8,128)S(1)}, u32[]{:S(2)}, u32[]{:S(2)}) collective-permute-start(f32[1,200,128]{2,1,0:T(8,128)S(1)} %get-tuple-element.46), channel_id=1, source_target_pairs={{0,8},{8,16},{16,24},{24,0},{1,9},{9,17},{17,25},{25,1},{2,10},{10... | collective-permute-start | bytes 307208 | tf_op jit(solution)/shard_map/ppermute | solution.py:14
  113.3 6.4 %collective-permute-start.5 = (f32[1,200,128]{2,1,0:T(8,128)S(1)}, f32[1,200,128]{2,1,0:T(8,128)S(1)}, u32[]{:S(2)}, u32[]{:S(2)}) collective-permute-start(f32[1,200,128]{2,1,0:T(8,128)S(1)} %get-tuple-element.45), channel_id=1, source_target_pairs={{0,1},{1,2},{2,3},{3,4},{4,5},{5,6},{6,7},{7,0},{8,9},{9,10},{10,1... | collective-permute-start | bytes 307208 | tf_op jit(solution)/shard_map/ppermute | solution.py:14
  119.7 0.8 copy-start.4
  120.9 5.5 %collective-permute-start.6 = (f32[2,2,3,128]{3,2,1,0:T(4,128)S(1)}, f32[2,2,3,128]{3,2,1,0:T(4,128)S(1)}, u32[]{:S(2)}, u32[]{:S(2)}) collective-permute-start(f32[2,2,3,128]{3,2,1,0:T(4,128)S(1)} %fusion.85), channel_id=1, source_target_pairs={{0,8},{8,16},{16,24},{24,0},{1,9},{9,17},{17,25},{25,1},{2,10},{10... | collective-permute-start | bytes 18440 | tf_op jit(solution)/shard_map/ppermute | solution.py:14
  127.0 4.2 collective-permute-start.7
  173.5 3.7 collective-permute-start.8
  177.8 2.0 collective-permute-start.9
  177.9 6.4 %copy-start.10 = (bf16[6,200,24]{1,0,2:T(8,128)(2,1)}, bf16[6,200,24]{1,0,2:T(8,128)(2,1)S(1)}, u32[]{:S(2)}) copy-start(bf16[6,200,24]{1,0,2:T(8,128)(2,1)S(1)} %dot_general.102) | copy-start | bytes 172804
  181.8 9.9 %copy-start.5 = (f32[1,1,1,3,200,128]{5,4,3,2,1,0:T(8,128)S(1)}, f32[1,1,1,3,200,128]{5,4,3,2,1,0:T(8,128)}, u32[]{:S(2)}) copy-start(f32[1,1,1,3,200,128]{5,4,3,2,1,0:T(8,128)} %param.7) | copy-start | bytes 921604
  181.8 9.9 %copy-start.13 = (f32[3]{0:T(128)S(1)}, f32[3]{0:T(128)}, u32[]{:S(2)}) copy-start(f32[3]{0:T(128)} %copy-done.12) | copy-start | bytes 40
  181.8 9.9 %copy-start.21 = (f32[3]{0:T(128)S(1)}, f32[3]{0:T(128)}, u32[]{:S(2)}) copy-start(f32[3]{0:T(128)} %copy-done.20) | copy-start | bytes 40
  182.3 49.7 %copy-start.14 = (f32[3]{0:T(128)S(1)}, f32[3]{0:T(128)}, u32[]{:S(2)}) copy-start(f32[3]{0:T(128)} %copy-done.12) | copy-start | bytes 40
  184.4 5.8 %collective-permute-start.10 = (f32[1,200,128]{2,1,0:T(8,128)S(1)}, f32[1,200,128]{2,1,0:T(8,128)S(1)}, u32[]{:S(2)}, u32[]{:S(2)}) collective-permute-start(f32[1,200,128]{2,1,0:T(8,128)S(1)} %get-tuple-element.29), channel_id=1, source_target_pairs={{0,24},{8,0},{16,8},{24,16},{1,25},{9,1},{17,9},{25,17},{2,26},{10... | collective-permute-start | bytes 307208 | tf_op jit(solution)/shard_map/ppermute | solution.py:14
  187.5 4.2 collective-permute-start.11
  231.4 57.3 %copy-start.18 = (f32[128]{0:T(128)}, f32[128]{0:T(128)S(1)}, u32[]{:S(2)}) copy-start(f32[128]{0:T(128)S(1)} %get-tuple-element.4) | copy-start | bytes 1540
  231.4 10.3 %copy-start.1 = (bf16[1,1,1,1200,1200]{4,3,2,1,0:T(8,128)(2,1)S(1)}, bf16[1,1,1,1200,1200]{4,3,2,1,0:T(8,128)(2,1)}, u32[]{:S(2)}) copy-start(bf16[1,1,1,1200,1200]{4,3,2,1,0:T(8,128)(2,1)} %param.9) | copy-start | bytes 8640004
  233.5 14.0 %copy-start.6 = (f32[3,200,128]{2,1,0:T(8,128)}, f32[3,200,128]{2,1,0:T(8,128)S(1)}, u32[]{:S(2)}) copy-start(f32[3,200,128]{2,1,0:T(8,128)S(1)} %get-tuple-element.13) | copy-start | bytes 921604
  234.4 6.5 %collective-permute-start.12 = (f32[1,200,128]{2,1,0:T(8,128)S(1)}, f32[1,200,128]{2,1,0:T(8,128)S(1)}, u32[]{:S(2)}, u32[]{:S(2)}) collective-permute-start(f32[1,200,128]{2,1,0:T(8,128)S(1)} %get-tuple-element.44), channel_id=1, source_target_pairs={{0,8},{8,16},{16,24},{24,0},{1,9},{9,17},{17,25},{25,1},{2,10},{10... | collective-permute-start | bytes 307208 | tf_op jit(solution)/shard_map/ppermute | solution.py:14
  236.6 5.0 %collective-permute-start.13 = (f32[1,200,128]{2,1,0:T(8,128)S(1)}, f32[1,200,128]{2,1,0:T(8,128)S(1)}, u32[]{:S(2)}, u32[]{:S(2)}) collective-permute-start(f32[1,200,128]{2,1,0:T(8,128)S(1)} %get-tuple-element.43), channel_id=1, source_target_pairs={{0,1},{1,2},{2,3},{3,4},{4,5},{5,6},{6,7},{7,0},{8,9},{9,10},{10,1... | collective-permute-start | bytes 307208 | tf_op jit(solution)/shard_map/ppermute | solution.py:14
  241.7 5.8 %copy-start.22 = (f32[3]{0:T(128)S(1)}, f32[3]{0:T(128)}, u32[]{:S(2)}) copy-start(f32[3]{0:T(128)} %copy-done.20) | copy-start | bytes 40
  242.7 107.9 %copy-start.9 = (f32[192,6]{1,0:T(8,128)S(1)}, f32[192,6]{1,0:T(8,128)}, u32[]{:S(2)}) copy-start(f32[192,6]{1,0:T(8,128)} %gather_fusion.1) | copy-start | bytes 13828
  242.7 4.7 %collective-permute-start.14 = (f32[1,200,128]{2,1,0:T(8,128)S(1)}, f32[1,200,128]{2,1,0:T(8,128)S(1)}, u32[]{:S(2)}, u32[]{:S(2)}) collective-permute-start(f32[1,200,128]{2,1,0:T(8,128)S(1)} %get-tuple-element.24), channel_id=1, source_target_pairs={{0,24},{8,0},{16,8},{24,16},{1,25},{9,1},{17,9},{25,17},{2,26},{10... | collective-permute-start | bytes 307208 | tf_op jit(solution)/shard_map/ppermute | solution.py:14
  244.5 3.0 collective-permute-start.15
  288.7 9.1 %copy-start.24 = (f32[128]{0:T(128)}, f32[128]{0:T(128)S(1)}, u32[]{:S(2)}) copy-start(f32[128]{0:T(128)S(1)} %psum.37) | copy-start | bytes 1540
  289.7 8.0 %copy-start.7 = (f32[3,200,128]{2,1,0:T(8,128)}, f32[3,200,128]{2,1,0:T(8,128)S(1)}, u32[]{:S(2)}) copy-start(f32[3,200,128]{2,1,0:T(8,128)S(1)} %get-tuple-element.11) | copy-start | bytes 921604
  290.7 6.5 %collective-permute-start.16 = (f32[1,200,128]{2,1,0:T(8,128)S(1)}, f32[1,200,128]{2,1,0:T(8,128)S(1)}, u32[]{:S(2)}, u32[]{:S(2)}) collective-permute-start(f32[1,200,128]{2,1,0:T(8,128)S(1)} %get-tuple-element.42), channel_id=1, source_target_pairs={{0,8},{8,16},{16,24},{24,0},{1,9},{9,17},{17,25},{25,1},{2,10},{10... | collective-permute-start | bytes 307208 | tf_op jit(solution)/shard_map/ppermute | solution.py:14
  292.7 5.0 %collective-permute-start.17 = (f32[1,200,128]{2,1,0:T(8,128)S(1)}, f32[1,200,128]{2,1,0:T(8,128)S(1)}, u32[]{:S(2)}, u32[]{:S(2)}) collective-permute-start(f32[1,200,128]{2,1,0:T(8,128)S(1)} %get-tuple-element.41), channel_id=1, source_target_pairs={{0,1},{1,2},{2,3},{3,4},{4,5},{5,6},{6,7},{7,0},{8,9},{9,10},{10,1... | collective-permute-start | bytes 307208 | tf_op jit(solution)/shard_map/ppermute | solution.py:14
  297.8 0.8 copy-start.3
  299.0 5.5 %collective-permute-start.18 = (f32[2,2,3,128]{3,2,1,0:T(4,128)S(1)}, f32[2,2,3,128]{3,2,1,0:T(4,128)S(1)}, u32[]{:S(2)}, u32[]{:S(2)}) collective-permute-start(f32[2,2,3,128]{3,2,1,0:T(4,128)S(1)} %fusion.83), channel_id=1, source_target_pairs={{0,8},{8,16},{16,24},{24,0},{1,9},{9,17},{17,25},{25,1},{2,10},{10... | collective-permute-start | bytes 18440 | tf_op jit(solution)/shard_map/ppermute | solution.py:14
  304.5 3.9 collective-permute-start.19
  351.9 3.7 collective-permute-start.20
  355.6 1.8 collective-permute-start.21
  357.5 9.4 %copy-start.8 = (f32[3,200,128]{2,1,0:T(8,128)S(1)}, f32[3,200,128]{2,1,0:T(8,128)}, u32[]{:S(2)}) copy-start(f32[3,200,128]{2,1,0:T(8,128)} %copy-done.7) | copy-start | bytes 921604
  357.5 9.4 %copy-start.15 = (f32[3]{0:T(128)S(1)}, f32[3]{0:T(128)}, u32[]{:S(2)}) copy-start(f32[3]{0:T(128)} %copy-done.12) | copy-start | bytes 40
  357.5 9.4 %copy-start.23 = (f32[3]{0:T(128)S(1)}, f32[3]{0:T(128)}, u32[]{:S(2)}) copy-start(f32[3]{0:T(128)} %copy-done.20) | copy-start | bytes 40
  358.9 47.7 %copy-start.25 = (f32[128]{0:T(128)S(1)}, f32[128]{0:T(128)}, u32[]{:S(2)}) copy-start(f32[128]{0:T(128)} %copy-done.24) | copy-start | bytes 1540
  358.9 47.7 %copy-start.17 = (f32[128]{0:T(128)S(1)}, f32[128]{0:T(128)}, u32[]{:S(2)}) copy-start(f32[128]{0:T(128)} %get-tuple-element.8) | copy-start | bytes 1540
  360.9 5.3 %collective-permute-start.22 = (f32[1,200,128]{2,1,0:T(8,128)S(1)}, f32[1,200,128]{2,1,0:T(8,128)S(1)}, u32[]{:S(2)}, u32[]{:S(2)}) collective-permute-start(f32[1,200,128]{2,1,0:T(8,128)S(1)} %get-tuple-element.19), channel_id=1, source_target_pairs={{0,24},{8,0},{16,8},{24,16},{1,25},{9,1},{17,9},{25,17},{2,26},{10... | collective-permute-start | bytes 307208 | tf_op jit(solution)/shard_map/ppermute | solution.py:14
  362.8 4.1 collective-permute-start.23
  406.6 10.3 %copy-start.2 = (bf16[1,1,1,1200,1200]{4,3,2,1,0:T(8,128)(2,1)S(1)}, bf16[1,1,1,1200,1200]{4,3,2,1,0:T(8,128)(2,1)}, u32[]{:S(2)}) copy-start(bf16[1,1,1,1200,1200]{4,3,2,1,0:T(8,128)(2,1)} %param.9) | copy-start | bytes 8640004
  409.6 6.5 %collective-permute-start.24 = (f32[1,200,128]{2,1,0:T(8,128)S(1)}, f32[1,200,128]{2,1,0:T(8,128)S(1)}, u32[]{:S(2)}, u32[]{:S(2)}) collective-permute-start(f32[1,200,128]{2,1,0:T(8,128)S(1)} %get-tuple-element.40), channel_id=1, source_target_pairs={{0,8},{8,16},{16,24},{24,0},{1,9},{9,17},{17,25},{25,1},{2,10},{10... | collective-permute-start | bytes 307208 | tf_op jit(solution)/shard_map/ppermute | solution.py:14
  411.8 5.0 %collective-permute-start.25 = (f32[1,200,128]{2,1,0:T(8,128)S(1)}, f32[1,200,128]{2,1,0:T(8,128)S(1)}, u32[]{:S(2)}, u32[]{:S(2)}) collective-permute-start(f32[1,200,128]{2,1,0:T(8,128)S(1)} %get-tuple-element.39), channel_id=1, source_target_pairs={{0,1},{1,2},{2,3},{3,4},{4,5},{5,6},{6,7},{7,0},{8,9},{9,10},{10,1... | collective-permute-start | bytes 307208 | tf_op jit(solution)/shard_map/ppermute | solution.py:14
  416.9 45.9 %copy-start.19 = (f32[128]{0:T(128)S(1)}, f32[128]{0:T(128)}, u32[]{:S(2)}) copy-start(f32[128]{0:T(128)} %copy-done.18) | copy-start | bytes 1540
  417.9 4.7 %collective-permute-start.26 = (f32[1,200,128]{2,1,0:T(8,128)S(1)}, f32[1,200,128]{2,1,0:T(8,128)S(1)}, u32[]{:S(2)}, u32[]{:S(2)}) collective-permute-start(f32[1,200,128]{2,1,0:T(8,128)S(1)} %get-tuple-element.14), channel_id=1, source_target_pairs={{0,24},{8,0},{16,8},{24,16},{1,25},{9,1},{17,9},{25,17},{2,26},{10... | collective-permute-start | bytes 307208 | tf_op jit(solution)/shard_map/ppermute | solution.py:14
  419.7 3.0 collective-permute-start.27
where the time goes:
time: 465 us; the launch traced here: 463 us
  blocking collectives  318 us (68%)
  waiting for transfers between devices  58.1 us (12%)
  matrix products  24.5 us (5%)
  starting transfers between devices  24.4 us (5%)
  other arithmetic  20.7 us (4%)
  local copies, waits for them, and re-layouts  16.7 us (4%)
    psum x3, blocking collectives, energy_total(): return lax.psum(partial_value, ('gx', 'gy'))  117 us
    all_gather x2, blocking collectives, local(): gathered = lax.all_gather(owned, ('gx', 'gy'), axis=0, tiled=True)  80 us
    ppermute x28, waiting for transfers between devices, passed_along(): lax.ppermute(array, axis, [(i, (i + by) % peers) for i in range(peers)])  58.1 us
    all_gather x1, blocking collectives, local(): lax.all_gather(coarse_inverse, ('gx', 'gy'), axis=0, tiled=True)  41.3 us
    unnamed x1, blocking collectives  40.4 us
    psum x1, blocking collectives, local(): curvature = lax.psum(inner_product(direction, product_field), ('gx', 'gy'))  38.5 us
    ppermute x28, starting transfers between devices, passed_along(): lax.ppermute(array, axis, [(i, (i + by) % peers) for i in range(peers)])  24.4 us
  transfers between devices with their start and end apart: 28, of which 20 were waited for; matrix products, arithmetic and copies ran while one was open for 4% of the time, Pallas kernels for 0%

commit v1 on v0

v1 whole, which is shorter than its diff:
```python
import functools

import jax
import jax.numpy as jnp
from jax import lax
from jax.experimental import pallas as pl
from jax.experimental.pallas import tpu as pltpu
from jax.sharding import PartitionSpec as P

ITERS = 2
EXCHANGES = 2 * ITERS
SUMS = 2 * ITERS + 1
GROUP = 32
MESH = pl.DeviceIdType.MESH
F32 = jnp.float32
BF16 = jnp.bfloat16


def split(value, parts):
    pieces = []
    for _ in range(parts):
        piece = value.astype(BF16)
        pieces.append(piece)
        value = value - piece.astype(F32)
    return pieces


def narrow_dot(matrix, value, parts):
    width = value.shape[1]
    product = jnp.dot(
        matrix, jnp.concatenate(split(value, parts), axis=1), preferred_element_type=F32
    )
    total = product[:, (parts - 1) * width :]
    for part in range(parts - 2, -1, -1):
        total = total + product[:, part * width : (part + 1) * width]
    return total


def full_dot(left, right):
    return jnp.dot(left, right, precision=lax.Precision.HIGHEST, preferred_element_type=F32)


def window(face, faces):
    start = face * faces // 128 * 128
    offset = face * faces - start
    return start, offset, -(-(offset + faces) // 128) * 128


def square_window(face, faces):
    start = face * faces // 128 * 128
    offset = face * faces - start
    return start, offset, -(-(offset + faces) // 256) * 256


def kernel(
    nx, ny, rhs_hbm, stiff_hbm, schur_hbm, phi_ref, cinv_ref, inc_ref, pair_ref,
    mult_ref, reduction_ref,
    rhs_v, stiff, schur, phi_f, phi_p, phi_t, near_t, near_phi, got_rhs, got_pair, got,
    field, way, image, sums_out, sums_in, ids_out, ids_in, cinv_in, cinv, chosen, assemble,
    load_out, load_in,
    local_sem, setup_send, setup_recv, face_send, face_recv, sum_send, sum_recv,
    all_send, all_recv, load_send, load_recv,
):
    n = nx * ny
    faces = rhs_v.shape[1]
    interface = stiff.shape[0]
    coarse = cinv.shape[0]
    ix, iy = lax.axis_index("gx"), lax.axis_index("gy")
    me = ix * ny + iy
    up_x, down_x = lax.rem(ix + 1, nx), lax.rem(ix + nx - 1, nx)
    up_y, down_y = lax.rem(iy + 1, ny), lax.rem(iy + ny - 1, ny)
    across = [(down_x, iy), (up_x, iy), (ix, down_y), (ix, up_y)]
    rows = [pl.ds(f * faces, faces) for f in range(6)]

    loads = [
        pltpu.make_async_copy(rhs_hbm, rhs_v, local_sem.at[0]),
        pltpu.make_async_copy(schur_hbm, schur, local_sem.at[1]),
        pltpu.make_async_copy(stiff_hbm, stiff, local_sem.at[2]),
    ]
    for copy in loads:
        copy.start()

    def peer(step):
        other = lax.rem(me + step, n)
        return (lax.div(other, ny), lax.rem(other, ny))

    barrier = pltpu.get_barrier_semaphore()

    def greet(step, carry):
        pl.semaphore_signal(barrier, inc=1, device_id=peer(step), device_id_type=MESH)
        return carry

    lax.fori_loop(1, n, greet, 0)

    corners = phi_f.shape[0]
    row = lax.broadcasted_iota(jnp.int32, (corners, corners), 0)
    col = lax.broadcasted_iota(jnp.int32, (corners, corners), 1)
    nodes = corners // 3
    order = jnp.where(col == 3 * lax.rem(row, nodes) + lax.div(row, nodes), 1.0, 0.0)
    phi_f[...] = jnp.dot(order.astype(BF16), phi_ref[...], preferred_element_type=F32)
    ids = jnp.broadcast_to(inc_ref[...].astype(F32), (nodes, nodes))
    diag = lax.broadcasted_iota(jnp.int32, (nodes, nodes), 0) == lax.broadcasted_iota(
        jnp.int32, (nodes, nodes), 1
    )
    ids = jnp.sum(jnp.where(diag, ids, 0.0), axis=1, keepdims=True)
    ids = jnp.broadcast_to(ids, ids_out.shape)
    ids_out[...] = ids
    ids_in[me] = ids
    cinv_in[me] = cinv_ref[...]

    loads[0].wait()
    pl.semaphore_wait(barrier, n - 1)

    def send(src, dst, send_sem, recv_sem, target):
        copy = pltpu.make_async_remote_copy(
            src_ref=src, dst_ref=dst, send_sem=send_sem, recv_sem=recv_sem,
            device_id=target, device_id_type=MESH,
        )
        copy.start()
        return copy

    def to_all(src, slots, send_sem, recv_sem):
        def step(k, carry):
            send(src, slots.at[me], send_sem, recv_sem, peer(k))
            return carry

        lax.fori_loop(1, n, step, 0)

    def wait_all(slots, sem):
        whole = slots.at[pl.ds(0, n - 1)]
        pltpu.make_async_copy(whole, whole, sem).wait()

    setup = []
    for a in range(2):
        setup.append(send(pair_ref, got_pair.at[a], setup_send.at[a], setup_recv.at[a],
                          across[2 * a + 1]))
    for a in range(2):
        setup.append(send(rhs_v.at[a], got_rhs.at[a], setup_send.at[2 + a],
                          setup_recv.at[2 + a], across[2 * a + 1]))
    for f in range(4):
        start, _, width = window(f, faces)
        partner = f ^ 1
        setup.append(send(phi_f.at[:, pl.ds(start, width)],
                          near_phi.at[partner, :, pl.ds(0, width)],
                          setup_send.at[4 + f], setup_recv.at[4 + partner], across[f]))
    to_all(ids_out, ids_in, all_send.at[0], all_recv.at[0])
    to_all(cinv_ref, cinv_in, all_send.at[1], all_recv.at[1])

    def turned(pair_row, offset, width):
        lanes = lax.broadcasted_iota(jnp.int32, (1, width), 1)
        if width > faces:
            pair_row = jnp.concatenate(
                [pair_row, jnp.zeros((1, width - faces), jnp.int32)], axis=1
            )
        if offset:
            pair_row = pltpu.roll(pair_row, offset, axis=1)
        inside = (lanes >= offset) & (lanes < offset + faces)
        target = jnp.where(inside, pair_row + offset, lanes)
        place = lax.broadcasted_iota(jnp.int32, (width, width), 0)
        return jnp.where(place == target, 1.0, 0.0)

    turns = []
    for a in range(2):
        setup[a].wait_recv()
        start, offset, width = square_window(2 * a, faces)
        by_col = turned(got_pair[a, a : a + 1, :], offset, width)
        turns.append((start, width, by_col.T.astype(BF16), by_col.astype(BF16)))

    def reorder(matrix):
        for start, width, by_row, _ in turns:
            band = matrix[pl.ds(start, width), :]
            matrix[pl.ds(start, width), :] = jnp.dot(
                by_row, band, preferred_element_type=F32
            ).astype(BF16)
        for start, width, _, by_col in turns:
            band = matrix[:, pl.ds(start, width)]
            matrix[:, pl.ds(start, width)] = jnp.dot(
                band, by_col, preferred_element_type=F32
            ).astype(BF16)

    loads[1].wait()
    reorder(schur)

    def apply_local(matrix, low, k):
        sent = []
        for half in range(3):
            part = pl.ds(2 * half * faces, 2 * faces)
            image[k, part, :] = jnp.dot(matrix[part, :], low, preferred_element_type=F32)
            if half < 2:
                for f in (2 * half, 2 * half + 1):
                    sent.append(send(image.at[k, rows[f]], got.at[k, f ^ 1],
                                     face_send.at[k, f], face_recv.at[k, f ^ 1], across[f]))
        return sent

    def start_sum(partial, k):
        total = jnp.sum(partial, axis=0, keepdims=True)
        sums_out[k] = total
        sums_in[k, me] = total
        to_all(sums_out.at[k], sums_in.at[k], sum_send.at[k], sum_recv.at[k])

    def finish_sum(k):
        wait_all(sums_in.at[k], sum_recv.at[k])
        return jnp.sum(sums_in[k], axis=0)

    def wait_faces(k):
        for f in range(4):
            pltpu.make_async_copy(got.at[k, f], got.at[k, f], face_recv.at[k, f]).wait()

    zeros = jnp.zeros((2 * faces, field.shape[1]), F32)
    for a in range(2):
        setup[2 + a].wait_recv()
        field[rows[2 * a], :] = -got_rhs[a]
        field[rows[2 * a + 1], :] = rhs_v[a]
    field[pl.ds(4 * faces, 2 * faces), :] = zeros
    for k in range(ITERS):
        way[k, pl.ds(4 * faces, 2 * faces), :] = zeros

    sent = []

    def precondition(k, s):
        half = 0.5 * field[...]
        sent.extend(apply_local(schur, half.astype(BF16), k))
        start_sum(half * image[k], s)

    precondition(0, 0)

    loads[2].wait()
    reorder(stiff)
    phi_p[...] = phi_f[...].astype(BF16)
    for start, width, _, by_col in turns:
        phi_p[:, pl.ds(start, width)] = jnp.dot(
            phi_p[:, pl.ds(start, width)], by_col, preferred_element_type=F32
        ).astype(BF16)
    phi_t[...] = phi_p[...].astype(F32).T.astype(BF16)

    def dof_rows(block):
        return jnp.concatenate([3.0 * block + i for i in range(3)], axis=block.ndim - 2)

    group = min(GROUP, n)

    def placed(g):
        block = dof_rows(ids_in[pl.ds(g * group, group)])
        line = block.reshape(group * corners, 128).T[0:1]
        spot = lax.broadcasted_iota(jnp.int32, (coarse, group * corners), 0).astype(F32)
        return jnp.where(spot == line, 1.0, 0.0).astype(BF16)

    def prepare_coarse():
        for f in range(4):
            _, offset, width = window(f ^ 1, faces)
            setup[4 + (f ^ 1)].wait_recv()
            tall = near_phi[f, :, pl.ds(0, width)].T[offset : offset + faces]
            if f % 2:
                by_row = turned(pair_ref[f // 2 : f // 2 + 1, :], 0, faces).T
                tall = jnp.dot(by_row.astype(BF16), tall.astype(BF16),
                               preferred_element_type=F32)
            near_t[f] = tall.astype(BF16)
        wait_all(ids_in, all_recv.at[0])
        if n == group:
            assemble[...] = placed(0)
        wait_all(cinv_in, all_recv.at[1])
        block_rows = cinv_in.shape[1]

        def pack(g, carry):
            block = jnp.concatenate([cinv_in[4 * g + i] for i in range(4)], axis=0)
            cinv[pl.ds(pl.multiple_of(4 * block_rows * g, 8), 4 * block_rows), :] = block
            return carry

        lax.fori_loop(0, n // 4, pack, 0)
        picks = []
        for gx, gy in across + [(ix, iy)]:
            dofs = dof_rows(ids_in[gx * ny + gy])[:, 0:1]
            spot = lax.broadcasted_iota(jnp.int32, (corners, coarse), 1).astype(F32)
            picks.append(jnp.where(spot == dofs, 1.0, 0.0))
        pick = jnp.concatenate(picks, axis=0).astype(BF16)
        chosen[...] = narrow_dot(pick, cinv[...], 3)

    energy = start_energy = previous = None
    alphas = []
    for it in range(ITERS):
        k = 2 * it
        wait_faces(k)
        if it:
            following = finish_sum(2 * it)
            ratio = following / energy
            energy = following
        for f in range(4):
            moved = 0.5 * (image[k, rows[f], :] - got[k, f])
            if it:
                moved = moved + ratio * way[it - 1, rows[f], :]
            way[it, rows[f], :] = moved
        walk = way[it]
        corner_load = narrow_dot(phi_p[...], walk, 2)
        load_out[it] = corner_load
        load_in[it, me] = corner_load
        to_all(load_out.at[it], load_in.at[it], load_send.at[it], load_recv.at[it])
        sent.extend(apply_local(stiff, walk.astype(BF16), k + 1))
        start_sum(walk * image[k + 1], 2 * it + 1)
        if it == 0:
            prepare_coarse()
            energy = start_energy = finish_sum(0)
        wait_all(load_in.at[it], load_recv.at[it])

        def gather(g, total):
            if n > group:
                assemble[...] = placed(g)
            block = load_in[it, pl.ds(g * group, group)].reshape(group * corners, -1)
            return total + narrow_dot(assemble[...], block, 3)

        coarse_load = lax.fori_loop(
            0, n // group, gather, jnp.zeros((coarse, field.shape[1]), F32)
        )
        solution_rows = full_dot(cinv[...], coarse_load)
        near = full_dot(chosen[...], coarse_load)
        coarse_part = jnp.sum(coarse_load * solution_rows, axis=0, keepdims=True)
        own = narrow_dot(phi_t[...], near[4 * corners :], 2)
        wait_faces(k + 1)
        alpha = energy / (finish_sum(2 * it + 1) + coarse_part)
        alphas.append(alpha)
        for f in range(4):
            other = narrow_dot(near_t[f], near[f * corners : (f + 1) * corners], 2)
            jump = (image[k + 1, rows[f], :] - got[k + 1, f]) + (
                own[f * faces : (f + 1) * faces] - other
            )
            field[rows[f], :] = field[rows[f], :] - alpha * jump
        if it + 1 < ITERS:
            precondition(k + 2, 2 * it + 2)
        else:
            half = 0.5 * field[...]
            product = jnp.dot(schur[...], half.astype(BF16), preferred_element_type=F32)
            start_sum(half * product, 2 * it + 2)

    for a in range(2):
        total = alphas[0] * way[0, rows[2 * a + 1], :]
        for it in range(1, ITERS):
            total = total + alphas[it] * way[it, rows[2 * a + 1], :]
        mult_ref[a] = total
    mult_ref[2] = jnp.zeros(mult_ref.shape[1:], F32)

    for copy in setup + sent:
        copy.wait_send()
    wait_all(ids_in, all_send.at[0])
    wait_all(cinv_in, all_send.at[1])
    for it in range(ITERS):
        wait_all(load_in.at[it], load_send.at[it])
    reduction_ref[...] = finish_sum(SUMS - 1) / start_energy
    for k in range(SUMS):
        wait_all(sums_in.at[k], sum_send.at[k])


def local(nx, ny, rhs, stiff_inverse, schur, phi, coarse_inverse, incidence, pairing):
    n = nx * ny
    faces, cases = rhs.shape[4], rhs.shape[5]
    interface = stiff_inverse.shape[3]
    corners = phi.shape[3]
    coarse_rows, coarse = coarse_inverse.shape
    nodes = incidence.shape[3]
    group = min(GROUP, n)
    wide = max(window(f, faces)[2] for f in range(4))
    vmem = pl.BlockSpec(memory_space=pltpu.VMEM)
    anywhere = pl.BlockSpec(memory_space=pl.ANY)
    dma = pltpu.SemaphoreType.DMA
    multipliers, reduction = pl.pallas_call(
        functools.partial(kernel, nx, ny),
        out_shape=(
            jax.ShapeDtypeStruct((3, faces, cases), F32),
            jax.ShapeDtypeStruct((1, cases), F32),
        ),
        in_specs=[anywhere] * 3 + [vmem] * 4,
        out_specs=(vmem, vmem),
        scratch_shapes=[
            pltpu.VMEM((3, faces, cases), F32),
            pltpu.VMEM((interface, interface), BF16),
            pltpu.VMEM((interface, interface), BF16),
            pltpu.VMEM((corners, interface), F32),
            pltpu.VMEM((corners, interface), BF16),
            pltpu.VMEM((interface, corners), BF16),
            pltpu.VMEM((4, faces, corners), BF16),
            pltpu.VMEM((4, corners, wide), F32),
            pltpu.VMEM((2, faces, cases), F32),
            pltpu.VMEM((2, 3, faces), jnp.int32),
            pltpu.VMEM((EXCHANGES, 4, faces, cases), F32),
            pltpu.VMEM((interface, cases), F32),
            pltpu.VMEM((ITERS, interface, cases), F32),
            pltpu.VMEM((EXCHANGES, interface, cases), F32),
            pltpu.VMEM((SUMS, 1, cases), F32),
            pltpu.VMEM((SUMS, n, 1, cases), F32),
            pltpu.VMEM((nodes, 128), F32),
            pltpu.VMEM((n, nodes, 128), F32),
            pltpu.VMEM((n, coarse_rows, coarse), F32),
            pltpu.VMEM((coarse, coarse), F32),
            pltpu.VMEM((5 * corners, coarse), F32),
            pltpu.VMEM((coarse, group * corners), BF16),
            pltpu.VMEM((ITERS, corners, cases), F32),
            pltpu.VMEM((ITERS, n, corners, cases), F32),
            dma((3,)),
            dma((8,)),
            dma((8,)),
            dma((EXCHANGES, 4)),
            dma((EXCHANGES, 4)),
            dma((SUMS,)),
            dma((SUMS,)),
            dma((2,)),
            dma((2,)),
            dma((ITERS,)),
            dma((ITERS,)),
        ],
        compiler_params=pltpu.CompilerParams(
            collective_id=0, has_side_effects=True, vmem_limit_bytes=67043328
        ),
    )(
        rhs.reshape(3, faces, cases),
        stiff_inverse.reshape(interface, interface),
        schur.reshape(interface, interface),
        phi.reshape(corners, interface),
        coarse_inverse,
        incidence.reshape(1, nodes),
        pairing.reshape(3, faces),
    )
    return multipliers.reshape(rhs.shape), reduction.reshape(cases)


def solution(mesh):
    nx, ny = mesh.shape["gx"], mesh.shape["gy"]
    return jax.shard_map(
        functools.partial(local, nx, ny),
        mesh=mesh,
        in_specs=(
            P("gx", "gy", None, None, None, None),
            P("gx", "gy", None, None, None),
            P("gx", "gy", None, None, None),
            P("gx", "gy", None, None, None),
            P(("gx", "gy"), None),
            P("gx", "gy", None, None),
            P("gx", "gy", None, None, None),
        ),
        out_specs=(P("gx", "gy", None, None, None, None), P()),
        check_vma=False,
    )
```

time: 465 us -> 80.4 us (0.17)
  blocking collectives: 318 us -> 0 us
  Pallas kernels: 0 us -> 75.4 us
  waiting for transfers between devices: 58.1 us -> 0 us
  matrix products: 24.5 us -> 0 us
  starting transfers between devices: 24.4 us -> 0 us
  other arithmetic: 20.7 us -> 0 us
  local copies, waits for them, and re-layouts: 16.7 us -> 4.17 us
    psum x4 -> x0, blocking collectives: 156 us -> none  [the longest x3 117 us: energy_total(): return lax.psum(partial_value, ('gx', 'gy'))]
    all_gather x3 -> x0, blocking collectives: 121 us -> none  [the longest x2 80 us: local(): gathered = lax.all_gather(owned, ('gx', 'gy'), axis=0, tiled=True)]
    pallas_call x0 -> x1, Pallas kernels: none -> 75.4 us  [local(): pl.pallas_call(functools.partial(kernel, nx, ny), out_shape=(jax.ShapeDty...]
    ppermute x28 -> x0, waiting for transfers between devices: 58.1 us -> none  [passed_along(): lax.ppermute(array, axis, [(i, (i + by) % peers) for i in range(peers)])]
    unnamed x1 -> x0, blocking collectives: 40.4 us -> none
    dot_general x21 -> x0, matrix products: 24.5 us -> none  [the longest x5 8.68 us: apply_local(): jnp.einsum('snm,smr->snr', matrices, low_field, preferred_element_type=jn...]
    ppermute x28 -> x0, starting transfers between devices: 24.4 us -> none  [passed_along(): lax.ppermute(array, axis, [(i, (i + by) % peers) for i in range(peers)])]
    mul x10 -> x0, other arithmetic: 8.42 us -> none  [the longest x6 6.5 us: transpose_jump(): masked = values * active]
  transfers between devices with their start and end apart: 28 -> 0, of which waited for: 20 -> 0; matrix products, arithmetic and copies ran while one was open for 4% -> 0% of each run, Pallas kernels for 0% -> 0%
where the time goes in v1:
time: 80.4 us; the launch traced here: 80.2 us
  Pallas kernels  75.4 us (94%)
  local copies, waits for them, and re-layouts  4.17 us (5%)
    pallas_call x1, Pallas kernels, local(): pl.pallas_call(functools.partial(kernel, nx, ny), out_shape=(jax.ShapeDty...  75.4 us
    unnamed x3, local copies, waits for them, and re-layouts  4.17 us

profile of v1, /device:TPU:0, one launch (start us, length us, event | category | flops | bytes accessed | tf_op | source)
XLA Modules:
  0.0 80.2 jit_solution(15039878468830973915)
XLA Ops:
  0.6 1.3 %copy.11 = s32[1,1,1,3,200]{4,3,2,1,0:T(4,128)} copy(s32[1,1,1,3,200]{4,2,3,1,0:T(1,128)} %param.13) | data formatting | bytes 4800
  1.9 75.4 %shard_map.86 = (f32[3,200,128]{2,1,0:T(8,128)}, f32[1,128]{1,0:T(1,128)}) custom-call(f32[3,200,128]{2,1,0:T(8,128)} %bitcast.13, bf16[1200,1200]{1,0:T(8,128)(2,1)} %bitcast.10, bf16[1200,1200]{1,0:T(8,128)(2,1)} %bitcast.11, bf16[24,1200]{1,0:T(8,128)(2,1)} %bitcast.14, f32[6,192]{1,0:T(8,128)} %cinv_ref.1, s32[1,8]{1,0:T(1,128)} %bitcast.16, ...), custom_call_target="tpu_custom_call" | custom-call | tf_op jit(solution)/shard_map/pallas_call | solution.py:362
  77.3 1.7 %copy.14 = f32[1,1,1,3,200,128]{5,4,3,2,1,0:T(8,128)} copy(f32[1,1,1,3,200,128]{5,4,3,2,1,0:T(8,128)} %bitcast.12) | data formatting | bytes 614400
  79.0 1.2 %copy.15 = f32[128]{0:T(128)} copy(f32[128]{0:T(128)} %bitcast.17) | data formatting | bytes 1024

commit v2 on v1

--- a/solution.py
+++ b/solution.py
@@ -10,7 +10,7 @@
 ITERS = 2
 EXCHANGES = 2 * ITERS
 SUMS = 2 * ITERS + 1
-GROUP = 32
+GROUP = 8
 MESH = pl.DeviceIdType.MESH
 F32 = jnp.float32
 BF16 = jnp.bfloat16
@@ -57,7 +57,7 @@
     mult_ref, reduction_ref,
     rhs_v, stiff, schur, phi_f, phi_p, phi_t, near_t, near_phi, got_rhs, got_pair, got,
     field, way, image, sums_out, sums_in, ids_out, ids_in, cinv_in, cinv, chosen, assemble,
-    load_out, load_in,
+    load_x, load_y,
     local_sem, setup_send, setup_recv, face_send, face_recv, sum_send, sum_recv,
     all_send, all_recv, load_send, load_recv,
 ):
@@ -80,33 +80,48 @@
     for copy in loads:
         copy.start()
 
-    def peer(step):
-        other = lax.rem(me + step, n)
-        return (lax.div(other, ny), lax.rem(other, ny))
+    ways_x = [ix] + [lax.rem(ix + d, nx) for d in range(1, nx)]
+    ways_y = [iy] + [lax.rem(iy + d, ny) for d in range(1, ny)]
+    peers_x = [(x, iy) for x in ways_x[1:]]
+    peers_y = [(ix, y) for y in ways_y[1:]]
+
+    def each_peer(act):
+        if n <= 64:
+            for x in range(nx):
+                for y in range(ny):
+                    if x or y:
+                        act((ways_x[x], ways_y[y]))
+            return
+
+        def step(k, carry):
+            other = lax.rem(me + k, n)
+            act((lax.div(other, ny), lax.rem(other, ny)))
+            return carry
+
+        lax.fori_loop(1, n, step, 0)
 
     barrier = pltpu.get_barrier_semaphore()
-
-    def greet(step, carry):
-        pl.semaphore_signal(barrier, inc=1, device_id=peer(step), device_id_type=MESH)
-        return carry
-
-    lax.fori_loop(1, n, greet, 0)
+    each_peer(lambda target: pl.semaphore_signal(
+        barrier, inc=1, device_id=target, device_id_type=MESH))
 
     corners = phi_f.shape[0]
     row = lax.broadcasted_iota(jnp.int32, (corners, corners), 0)
     col = lax.broadcasted_iota(jnp.int32, (corners, corners), 1)
     nodes = corners // 3
-    order = jnp.where(col == 3 * lax.rem(row, nodes) + lax.div(row, nodes), 1.0, 0.0)
+    side, half_rows = nodes // 2, corners // 2
+    inner = lax.rem(row, half_rows)
+    corner = lax.div(row, half_rows) + 2 * lax.rem(inner, side)
+    order = jnp.where(col == 3 * corner + lax.div(inner, side), 1.0, 0.0)
     phi_f[...] = jnp.dot(order.astype(BF16), phi_ref[...], preferred_element_type=F32)
     ids = jnp.broadcast_to(inc_ref[...].astype(F32), (nodes, nodes))
-    diag = lax.broadcasted_iota(jnp.int32, (nodes, nodes), 0) == lax.broadcasted_iota(
-        jnp.int32, (nodes, nodes), 1
-    )
+    row = lax.broadcasted_iota(jnp.int32, (nodes, nodes), 0)
+    col = lax.broadcasted_iota(jnp.int32, (nodes, nodes), 1)
+    diag = col == lax.div(row, side) + 2 * lax.rem(row, side)
     ids = jnp.sum(jnp.where(diag, ids, 0.0), axis=1, keepdims=True)
     ids = jnp.broadcast_to(ids, ids_out.shape)
     ids_out[...] = ids
-    ids_in[me] = ids
-    cinv_in[me] = cinv_ref[...]
+    ids_in[iy, ix] = ids
+    cinv_in[iy, ix] = cinv_ref[...]
 
     loads[0].wait()
     pl.semaphore_wait(barrier, n - 1)
@@ -120,14 +135,14 @@
         return copy
 
     def to_all(src, slots, send_sem, recv_sem):
-        def step(k, carry):
-            send(src, slots.at[me], send_sem, recv_sem, peer(k))
-            return carry
-
-        lax.fori_loop(1, n, step, 0)
+        each_peer(lambda target: send(src, slots.at[me], send_sem, recv_sem, target))
+
+    def to_line(src, dst, send_sem, recv_sem, targets):
+        for target in targets:
+            send(src, dst, send_sem, recv_sem, target)
 
     def wait_all(slots, sem):
-        whole = slots.at[pl.ds(0, n - 1)]
+        whole = slots.at[pl.ds(0, slots.shape[0] - 1)]
         pltpu.make_async_copy(whole, whole, sem).wait()
 
     setup = []
@@ -143,8 +158,8 @@
         setup.append(send(phi_f.at[:, pl.ds(start, width)],
                           near_phi.at[partner, :, pl.ds(0, width)],
                           setup_send.at[4 + f], setup_recv.at[4 + partner], across[f]))
-    to_all(ids_out, ids_in, all_send.at[0], all_recv.at[0])
-    to_all(cinv_ref, cinv_in, all_send.at[1], all_recv.at[1])
+    to_line(ids_out, ids_in.at[iy, ix], all_send.at[0], all_recv.at[0], peers_x)
+    to_line(cinv_ref, cinv_in.at[iy, ix], all_send.at[1], all_recv.at[1], peers_x)
 
     def turned(pair_row, offset, width):
         lanes = lax.broadcasted_iota(jnp.int32, (1, width), 1)
@@ -178,6 +193,10 @@
                 band, by_col, preferred_element_type=F32
             ).astype(BF16)
 
+    wait_all(ids_in.at[iy], all_recv.at[0])
+    wait_all(cinv_in.at[iy], all_recv.at[1])
+    to_line(ids_in.at[iy], ids_in.at[iy], all_send.at[2], all_recv.at[2], peers_y)
+    to_line(cinv_in.at[iy], cinv_in.at[iy], all_send.at[3], all_recv.at[3], peers_y)
     loads[1].wait()
     reorder(schur)
 
@@ -233,15 +252,22 @@
         ).astype(BF16)
     phi_t[...] = phi_p[...].astype(F32).T.astype(BF16)
 
+    group = min(GROUP, ny)
+    width = nx * half_rows
+
     def dof_rows(block):
-        return jnp.concatenate([3.0 * block + i for i in range(3)], axis=block.ndim - 2)
-
-    group = min(GROUP, n)
+        return jnp.concatenate(
+            [3.0 * block[h * side : (h + 1) * side] + i for h in range(2) for i in range(3)],
+            axis=0,
+        )
 
     def placed(g):
-        block = dof_rows(ids_in[pl.ds(g * group, group)])
-        line = block.reshape(group * corners, 128).T[0:1]
-        spot = lax.broadcasted_iota(jnp.int32, (coarse, group * corners), 0).astype(F32)
+        block = ids_in[pl.ds(g * group, group)].reshape(group * nx // 2, 2, nodes, 128)
+        block = jnp.concatenate(
+            [3.0 * block[:, b, 0:side] + i for b in range(2) for i in range(3)], axis=1
+        )
+        line = block.reshape(group * width, 128).T[0:1]
+        spot = lax.broadcasted_iota(jnp.int32, (coarse, group * width), 0).astype(F32)
         return jnp.where(spot == line, 1.0, 0.0).astype(BF16)
 
     def prepare_coarse():
@@ -254,21 +280,22 @@
                 tall = jnp.dot(by_row.astype(BF16), tall.astype(BF16),
                                preferred_element_type=F32)
             near_t[f] = tall.astype(BF16)
-        wait_all(ids_in, all_recv.at[0])
-        if n == group:
+        wait_all(ids_in, all_recv.at[2])
+        if ny == group:
             assemble[...] = placed(0)
-        wait_all(cinv_in, all_recv.at[1])
-        block_rows = cinv_in.shape[1]
-
-        def pack(g, carry):
-            block = jnp.concatenate([cinv_in[4 * g + i] for i in range(4)], axis=0)
-            cinv[pl.ds(pl.multiple_of(4 * block_rows * g, 8), 4 * block_rows), :] = block
-            return carry
-
-        lax.fori_loop(0, n // 4, pack, 0)
+        wait_all(cinv_in, all_recv.at[3])
+        block_rows = 4 * cinv_in.shape[2]
+        for x in range(nx):
+            def pack(g, carry):
+                block = jnp.concatenate([cinv_in[4 * g + i, x] for i in range(4)], axis=0)
+                place = (x * (ny // 4) + g) * block_rows
+                cinv[pl.ds(pl.multiple_of(place, 8), block_rows), :] = block
+                return carry
+
+            lax.fori_loop(0, ny // 4, pack, 0, unroll=ny <= 8)
         picks = []
         for gx, gy in across + [(ix, iy)]:
-            dofs = dof_rows(ids_in[gx * ny + gy])[:, 0:1]
+            dofs = dof_rows(ids_in[gy, gx])[:, 0:1]
             spot = lax.broadcasted_iota(jnp.int32, (corners, coarse), 1).astype(F32)
             picks.append(jnp.where(spot == dofs, 1.0, 0.0))
         pick = jnp.concatenate(picks, axis=0).astype(BF16)
@@ -290,24 +317,33 @@
             way[it, rows[f], :] = moved
         walk = way[it]
         corner_load = narrow_dot(phi_p[...], walk, 2)
-        load_out[it] = corner_load
-        load_in[it, me] = corner_load
-        to_all(load_out.at[it], load_in.at[it], load_send.at[it], load_recv.at[it])
+        load_x[it, ix] = corner_load
+        to_line(load_x.at[it, ix], load_x.at[it, ix], load_send.at[it], load_recv.at[it],
+                peers_x)
         sent.extend(apply_local(stiff, walk.astype(BF16), k + 1))
         start_sum(walk * image[k + 1], 2 * it + 1)
+        wait_all(load_x.at[it], load_recv.at[it])
+        for pair in range(nx // 2):
+            joined = [
+                load_x[it, x, 0:half_rows] + load_x[it, (x - 1) % nx, half_rows:corners]
+                for x in (2 * pair, 2 * pair + 1)
+            ]
+            load_y[it, iy, pl.ds(pair * corners, corners)] = jnp.concatenate(joined, axis=0)
+        to_line(load_y.at[it, iy], load_y.at[it, iy], load_send.at[ITERS + it],
+                load_recv.at[ITERS + it], peers_y)
         if it == 0:
             prepare_coarse()
             energy = start_energy = finish_sum(0)
-        wait_all(load_in.at[it], load_recv.at[it])
+        wait_all(load_y.at[it], load_recv.at[ITERS + it])
 
         def gather(g, total):
-            if n > group:
+            if ny > group:
                 assemble[...] = placed(g)
-            block = load_in[it, pl.ds(g * group, group)].reshape(group * corners, -1)
+            block = load_y[it, pl.ds(g * group, group)].reshape(group * width, -1)
             return total + narrow_dot(assemble[...], block, 3)
 
         coarse_load = lax.fori_loop(
-            0, n // group, gather, jnp.zeros((coarse, field.shape[1]), F32)
+            0, ny // group, gather, jnp.zeros((coarse, field.shape[1]), F32)
         )
         solution_rows = full_dot(cinv[...], coarse_load)
         near = full_dot(chosen[...], coarse_load)
@@ -338,10 +374,13 @@
 
     for copy in setup + sent:
         copy.wait_send()
-    wait_all(ids_in, all_send.at[0])
-    wait_all(cinv_in, all_send.at[1])
+    wait_all(ids_in.at[iy], all_send.at[0])
+    wait_all(cinv_in.at[iy], all_send.at[1])
+    wait_all(ids_in, all_send.at[2])
+    wait_all(cinv_in, all_send.at[3])
     for it in range(ITERS):
-        wait_all(load_in.at[it], load_send.at[it])
+        wait_all(load_x.at[it], load_send.at[it])
+        wait_all(load_y.at[it], load_send.at[ITERS + it])
     reduction_ref[...] = finish_sum(SUMS - 1) / start_energy
     for k in range(SUMS):
         wait_all(sums_in.at[k], sum_send.at[k])
@@ -354,7 +393,7 @@
     corners = phi.shape[3]
     coarse_rows, coarse = coarse_inverse.shape
     nodes = incidence.shape[3]
-    group = min(GROUP, n)
+    group = min(GROUP, ny)
     wide = max(window(f, faces)[2] for f in range(4))
     vmem = pl.BlockSpec(memory_space=pltpu.VMEM)
     anywhere = pl.BlockSpec(memory_space=pl.ANY)
@@ -385,13 +424,13 @@
             pltpu.VMEM((SUMS, 1, cases), F32),
             pltpu.VMEM((SUMS, n, 1, cases), F32),
             pltpu.VMEM((nodes, 128), F32),
-            pltpu.VMEM((n, nodes, 128), F32),
-            pltpu.VMEM((n, coarse_rows, coarse), F32),
+            pltpu.VMEM((ny, nx, nodes, 128), F32),
+            pltpu.VMEM((ny, nx, coarse_rows, coarse), F32),
             pltpu.VMEM((coarse, coarse), F32),
             pltpu.VMEM((5 * corners, coarse), F32),
-            pltpu.VMEM((coarse, group * corners), BF16),
-            pltpu.VMEM((ITERS, corners, cases), F32),
-            pltpu.VMEM((ITERS, n, corners, cases), F32),
+            pltpu.VMEM((coarse, group * nx * corners // 2), BF16),
+            pltpu.VMEM((ITERS, nx, corners, cases), F32),
+            pltpu.VMEM((ITERS, ny, nx * corners // 2, cases), F32),
             dma((3,)),
             dma((8,)),
             dma((8,)),
@@ -399,10 +438,10 @@
             dma((EXCHANGES, 4)),
             dma((SUMS,)),
             dma((SUMS,)),
-            dma((2,)),
-            dma((2,)),
-            dma((ITERS,)),
-            dma((ITERS,)),
+            dma((4,)),
+            dma((4,)),
+            dma((2 * ITERS,)),
+            dma((2 * ITERS,)),
         ],
         compiler_params=pltpu.CompilerParams(
             collective_id=0, has_side_effects=True, vmem_limit_bytes=67043328

time: 80.4 us -> 65.2 us (0.81)
  Pallas kernels: 75.4 us -> 60.2 us
    pallas_call x1, Pallas kernels: 75.4 us -> 60.2 us  [local(): pl.pallas_call(functools.partial(kernel, nx, ny), out_shape=(jax.ShapeDty...]
where the time goes in v2:
time: 65.2 us; the launch traced here: 65 us
  Pallas kernels  60.2 us (92%)
  local copies, waits for them, and re-layouts  4.17 us (6%)
    pallas_call x1, Pallas kernels, local(): pl.pallas_call(functools.partial(kernel, nx, ny), out_shape=(jax.ShapeDty...  60.2 us
    unnamed x3, local copies, waits for them, and re-layouts  4.17 us

profile of v2, /device:TPU:0, one launch (start us, length us, event | category | flops | bytes accessed | tf_op | source)
XLA Modules:
  0.0 65.0 jit_solution(13163209788840468170)
XLA Ops:
  0.6 1.3 %copy.11 = s32[1,1,1,3,200]{4,3,2,1,0:T(4,128)} copy(s32[1,1,1,3,200]{4,2,3,1,0:T(1,128)} %param.13) | data formatting | bytes 4800
  1.9 60.2 %shard_map.86 = (f32[3,200,128]{2,1,0:T(8,128)}, f32[1,128]{1,0:T(1,128)}) custom-call(f32[3,200,128]{2,1,0:T(8,128)} %bitcast.13, bf16[1200,1200]{1,0:T(8,128)(2,1)} %bitcast.10, bf16[1200,1200]{1,0:T(8,128)(2,1)} %bitcast.11, bf16[24,1200]{1,0:T(8,128)(2,1)} %bitcast.14, f32[6,192]{1,0:T(8,128)} %cinv_ref.1, s32[1,8]{1,0:T(1,128)} %bitcast.16, ...), custom_call_target="tpu_custom_call" | custom-call | tf_op jit(solution)/shard_map/pallas_call | solution.py:401
  62.1 1.7 %copy.14 = f32[1,1,1,3,200,128]{5,4,3,2,1,0:T(8,128)} copy(f32[1,1,1,3,200,128]{5,4,3,2,1,0:T(8,128)} %bitcast.12) | data formatting | bytes 614400
  63.8 1.2 %copy.15 = f32[128]{0:T(128)} copy(f32[128]{0:T(128)} %bitcast.17) | data formatting | bytes 1024

commit v3 on v2

--- a/solution.py
+++ b/solution.py
@@ -321,7 +321,6 @@
         to_line(load_x.at[it, ix], load_x.at[it, ix], load_send.at[it], load_recv.at[it],
                 peers_x)
         sent.extend(apply_local(stiff, walk.astype(BF16), k + 1))
-        start_sum(walk * image[k + 1], 2 * it + 1)
         wait_all(load_x.at[it], load_recv.at[it])
         for pair in range(nx // 2):
             joined = [
@@ -331,6 +330,7 @@
             load_y[it, iy, pl.ds(pair * corners, corners)] = jnp.concatenate(joined, axis=0)
         to_line(load_y.at[it, iy], load_y.at[it, iy], load_send.at[ITERS + it],
                 load_recv.at[ITERS + it], peers_y)
+        start_sum(walk * image[k + 1], 2 * it + 1)
         if it == 0:
             prepare_coarse()
             energy = start_energy = finish_sum(0)

time: 65.2 us -> 65.2 us (level)
  no operation moved by 1% of the time
where the time goes in v3:
time: 65.2 us; the launch traced here: 65 us
  Pallas kernels  60.2 us (92%)
  local copies, waits for them, and re-layouts  4.17 us (6%)
    pallas_call x1, Pallas kernels, local(): pl.pallas_call(functools.partial(kernel, nx, ny), out_shape=(jax.ShapeDty...  60.2 us
    unnamed x3, local copies, waits for them, and re-layouts  4.17 us

profile of v3, /device:TPU:0, one launch (start us, length us, event | category | flops | bytes accessed | tf_op | source)
XLA Modules:
  0.0 65.0 jit_solution(2784138029685316558)
XLA Ops:
  0.6 1.3 %copy.11 = s32[1,1,1,3,200]{4,3,2,1,0:T(4,128)} copy(s32[1,1,1,3,200]{4,2,3,1,0:T(1,128)} %param.13) | data formatting | bytes 4800
  1.9 60.2 %shard_map.86 = (f32[3,200,128]{2,1,0:T(8,128)}, f32[1,128]{1,0:T(1,128)}) custom-call(f32[3,200,128]{2,1,0:T(8,128)} %bitcast.13, bf16[1200,1200]{1,0:T(8,128)(2,1)} %bitcast.10, bf16[1200,1200]{1,0:T(8,128)(2,1)} %bitcast.11, bf16[24,1200]{1,0:T(8,128)(2,1)} %bitcast.14, f32[6,192]{1,0:T(8,128)} %cinv_ref.1, s32[1,8]{1,0:T(1,128)} %bitcast.16, ...), custom_call_target="tpu_custom_call" | custom-call | tf_op jit(solution)/shard_map/pallas_call | solution.py:401
  62.1 1.7 %copy.14 = f32[1,1,1,3,200,128]{5,4,3,2,1,0:T(8,128)} copy(f32[1,1,1,3,200,128]{5,4,3,2,1,0:T(8,128)} %bitcast.12) | data formatting | bytes 614400
  63.8 1.2 %copy.15 = f32[128]{0:T(128)} copy(f32[128]{0:T(128)} %bitcast.17) | data formatting | bytes 1024
